TPU v7x, 32 devices: a whole 2x2x4 slice. The times are simulated.
32 devices in a mesh: row: 8 (over z, y), col: 4 (over x, core).
Axes of the slice: x: 2, y: 2, z: 4, core: 2. Of those that a mesh axis runs over, the one named last changes fastest.
Arguments:
- hidden: bfloat16 [131072, 1024], P(('row', 'col')), may hold values from -6 to 6
- routes: int32 [64, 256], P(('row', 'col')), may hold values from 0 to 2047, as said below
- w_qkv: bfloat16 [1024, 3072], P('row', 'col'), may hold values from -0.1875 to 0.1875
- w_proj: bfloat16 [1024, 1024], P('row', 'col'), may hold values from -0.75 to 0.75
- w_up: bfloat16 [1024, 4096], P('row', 'col'), may hold values from -0.1875 to 0.1875
- w_down: bfloat16 [4096, 1024], P('row', 'col'), may hold values from -0.09375 to 0.09375
- attn_gain: bfloat16 [1024], P(('row', 'col')), may hold values from 0.5 to 1.5
- mlp_gain: bfloat16 [1024], P(('row', 'col')), may hold values from 0.5 to 1.5
- router: bfloat16 [1024], P(('row', 'col')), may hold values from -0.1875 to 0.1875
- cotangent: bfloat16 [131072, 1024], P(('row', 'col')), may hold values from -6 to 6
Outputs:
- layer_out: bfloat16 [131072, 1024], P(('row', 'col'))
- grad_hidden: float32 [131072, 1024], P(('row', 'col'))
- grad_qkv: float32 [1024, 3072], P('row', 'col')
- grad_proj: float32 [1024, 1024], P('row', 'col')
- grad_up: float32 [1024, 4096], P('row', 'col')
- grad_down: float32 [4096, 1024], P('row', 'col')
- grad_attngain: float32 [1024], P(('row', 'col'))
- grad_mlpgain: float32 [1024], P(('row', 'col'))
- grad_router: float32 [1024], P(('row', 'col'))
Inputs may be any that keep to these rules, and one draw needn't show every extreme that they name: `routes`: each row lists 256 distinct positions of its sequence in increasing order.
All inputs are finite; a program needn't handle non-finite values.
Results may differ from a plain program's by a relative error of at most 0.019.
Values may be sent and summed in bfloat16 or wider, within the bound.
No kernel may reach another device: no remote copies, remote signals or barrier semaphores. Data moves between devices by JAX's collectives and lax.ppermute only.
A program may use at most 320 MiB of HBM per device.

v0:
```python
import jax
import jax.numpy as jnp
from jax import lax
from jax.sharding import PartitionSpec as P

HEADS = 16
HEAD_DIM = 64
L = 2048
BLOCK = 256


epsilon = 1e-05
sqrt_half = 0.7071067811865476
inv_root_two_pi = 0.3989422804014327


def gelu_slope(value):
    return (
        0.5 * (1.0 + lax.erf(value * sqrt_half))
        + value * jnp.exp(-0.5 * value * value) * inv_root_two_pi
    )


def one_sequence(weights, sequence, picked, seq_cot):
    qkv_mat, proj_mat, up_mat, down_mat, gain_attn, gain_mlp, router_vec = weights
    count = picked.shape[0]
    width = sequence.shape[1]
    scale = HEAD_DIM ** (-0.5)
    routed = jnp.take(sequence, picked, axis=0).astype(jnp.float32)
    gating = jax.nn.sigmoid(jnp.dot(routed, router_vec, precision=lax.Precision.HIGHEST))
    inv_first = lax.rsqrt(jnp.mean(routed * routed, axis=-1, keepdims=True) + epsilon)
    unit_first = routed * inv_first
    normed = (unit_first * gain_attn).astype(jnp.bfloat16)
    projected = jnp.dot(normed, qkv_mat, preferred_element_type=jnp.float32).astype(jnp.bfloat16)
    split = projected.reshape(count, 3, HEADS, HEAD_DIM).transpose(1, 2, 0, 3)
    query, keys, values = (split[0], split[1], split[2])
    scores = jnp.einsum("hqd,hkd->hqk", query, keys, preferred_element_type=jnp.float32) * scale
    blocks = picked // BLOCK
    allowed = blocks[:, None] >= blocks[None, :]
    masked = jnp.where(allowed[None], scores, -1e30)
    row_top = jnp.max(masked, axis=-1, keepdims=True)
    expo = jnp.exp(masked - row_top)
    probs = expo / jnp.sum(expo, axis=-1, keepdims=True)
    probs_low = probs.astype(jnp.bfloat16)
    mixed = jnp.einsum("hqk,hkd->hqd", probs_low, values, preferred_element_type=jnp.float32)
    mixed_low = mixed.transpose(1, 0, 2).reshape(count, width).astype(jnp.bfloat16)
    attn_out = jnp.dot(mixed_low, proj_mat, preferred_element_type=jnp.float32)
    resid = routed + attn_out
    inv_second = lax.rsqrt(jnp.mean(resid * resid, axis=-1, keepdims=True) + epsilon)
    unit_second = resid * inv_second
    normed_two = (unit_second * gain_mlp).astype(jnp.bfloat16)
    pre_act = jnp.dot(normed_two, up_mat, preferred_element_type=jnp.float32)
    act_low = jax.nn.gelu(pre_act, approximate=False).astype(jnp.bfloat16)
    mlp_out = jnp.dot(act_low, down_mat, preferred_element_type=jnp.float32)
    branch = attn_out + mlp_out
    updated = routed + gating[:, None] * branch
    result = sequence.at[picked].set(updated.astype(jnp.bfloat16))
    grad_routed_out = jnp.take(seq_cot, picked, axis=0).astype(jnp.float32)
    grad_gating = jnp.sum(grad_routed_out * branch, axis=-1)
    grad_score = grad_gating * gating * (1.0 - gating)
    grad_router_vec = jnp.dot(grad_score, routed, precision=lax.Precision.HIGHEST)
    grad_rows = grad_routed_out + grad_score[:, None] * router_vec[None, :]
    grad_branch = gating[:, None] * grad_routed_out
    grad_mlp = grad_branch.astype(jnp.bfloat16)
    grad_act = jnp.dot(grad_mlp, down_mat.T, preferred_element_type=jnp.float32)
    grad_down_mat = jnp.dot(act_low.T, grad_mlp, preferred_element_type=jnp.float32)
    grad_pre = (grad_act * gelu_slope(pre_act)).astype(jnp.bfloat16)
    grad_normed_two = jnp.dot(grad_pre, up_mat.T, preferred_element_type=jnp.float32)
    grad_up_mat = jnp.dot(normed_two.T, grad_pre, preferred_element_type=jnp.float32)
    grad_gain_mlp = jnp.sum(grad_normed_two * unit_second, axis=0)
    scaled_two = grad_normed_two * gain_mlp
    grad_resid = inv_second * (
        scaled_two - unit_second * jnp.mean(scaled_two * unit_second, axis=-1, keepdims=True)
    )
    grad_attn = (grad_branch + grad_resid).astype(jnp.bfloat16)
    grad_rows = grad_rows + grad_resid
    grad_mixed = jnp.dot(grad_attn, proj_mat.T, preferred_element_type=jnp.float32).astype(
        jnp.bfloat16
    )
    grad_proj_mat = jnp.dot(mixed_low.T, grad_attn, preferred_element_type=jnp.float32)
    grad_heads = grad_mixed.reshape(count, HEADS, HEAD_DIM).transpose(1, 0, 2)
    grad_probs = jnp.einsum("hqd,hkd->hqk", grad_heads, values, preferred_element_type=jnp.float32)
    grad_values = jnp.einsum(
        "hqk,hqd->hkd", probs_low, grad_heads, preferred_element_type=jnp.float32
    )
    grad_scores = probs * (grad_probs - jnp.sum(probs * grad_probs, axis=-1, keepdims=True))
    grad_scores = grad_scores.astype(jnp.bfloat16)
    grad_query = (
        jnp.einsum("hqk,hkd->hqd", grad_scores, keys, preferred_element_type=jnp.float32) * scale
    )
    grad_keys = (
        jnp.einsum("hqk,hqd->hkd", grad_scores, query, preferred_element_type=jnp.float32) * scale
    )
    grad_projected = jnp.stack([grad_query, grad_keys, grad_values]).transpose(2, 0, 1, 3)
    grad_projected = grad_projected.reshape(count, 3 * width).astype(jnp.bfloat16)
    grad_normed = jnp.dot(grad_projected, qkv_mat.T, preferred_element_type=jnp.float32)
    grad_qkv_mat = jnp.dot(normed.T, grad_projected, preferred_element_type=jnp.float32)
    grad_gain_attn = jnp.sum(grad_normed * unit_first, axis=0)
    scaled_one = grad_normed * gain_attn
    grad_rows = grad_rows + inv_first * (
        scaled_one - unit_first * jnp.mean(scaled_one * unit_first, axis=-1, keepdims=True)
    )
    grad_sequence = seq_cot.astype(jnp.float32).at[picked].set(grad_rows)
    grads = (
        grad_qkv_mat,
        grad_proj_mat,
        grad_up_mat,
        grad_down_mat,
        grad_gain_attn,
        grad_gain_mlp,
        grad_router_vec,
    )
    return (result, grad_sequence, grads)


def on_device(hidden, routes, w_qkv, w_proj, w_up, w_down, attn_gain, mlp_gain, router, cotangent):
    across = (
        lax.all_gather(w_qkv, "col", axis=1, tiled=True),
        lax.all_gather(w_proj, "col", axis=1, tiled=True),
        lax.all_gather(w_up, "col", axis=1, tiled=True),
        lax.all_gather(w_down, "col", axis=1, tiled=True),
        lax.all_gather(attn_gain.reshape(1, -1), "col", axis=1, tiled=True),
        lax.all_gather(mlp_gain.reshape(1, -1), "col", axis=1, tiled=True),
        lax.all_gather(router.reshape(1, -1), "col", axis=1, tiled=True),
    )
    gathered = (
        lax.all_gather(across[0], "row", axis=0, tiled=True),
        lax.all_gather(across[1], "row", axis=0, tiled=True),
        lax.all_gather(across[2], "row", axis=0, tiled=True),
        lax.all_gather(across[3], "row", axis=0, tiled=True),
        lax.all_gather(across[4], "row", axis=0, tiled=True),
        lax.all_gather(across[5], "row", axis=0, tiled=True),
        lax.all_gather(across[6], "row", axis=0, tiled=True),
    )
    weights = (
        gathered[0],
        gathered[1],
        gathered[2],
        gathered[3],
        gathered[4].reshape(-1).astype(jnp.float32),
        gathered[5].reshape(-1).astype(jnp.float32),
        gathered[6].reshape(-1).astype(jnp.float32),
    )
    width = hidden.shape[1]
    sequences = hidden.shape[0] // L
    zeros = (
        jnp.zeros(weights[0].shape, jnp.float32),
        jnp.zeros(weights[1].shape, jnp.float32),
        jnp.zeros(weights[2].shape, jnp.float32),
        jnp.zeros(weights[3].shape, jnp.float32),
        jnp.zeros((width,), jnp.float32),
        jnp.zeros((width,), jnp.float32),
        jnp.zeros((width,), jnp.float32),
    )

    def visit(carried, item):
        sequence, picked, seq_cot = item
        result, grad_sequence, grads = one_sequence(weights, sequence, picked, seq_cot)
        carried = tuple((older + newer for older, newer in zip(carried, grads)))
        return (carried, (result, grad_sequence))

    totals, (outputs, grads_seq) = lax.scan(
        visit,
        zeros,
        (hidden.reshape(sequences, L, width), routes, cotangent.reshape(sequences, L, width)),
    )
    n_rows = lax.axis_size("row")
    first_pass = (
        lax.psum_scatter(
            totals[0].astype(jnp.bfloat16), "row", scatter_dimension=0, tiled=True
        ).astype(jnp.float32),
        lax.psum_scatter(
            totals[1].astype(jnp.bfloat16), "row", scatter_dimension=0, tiled=True
        ).astype(jnp.float32),
        lax.psum_scatter(
            totals[2].astype(jnp.bfloat16), "row", scatter_dimension=0, tiled=True
        ).astype(jnp.float32),
        lax.psum_scatter(
            totals[3].astype(jnp.bfloat16), "row", scatter_dimension=0, tiled=True
        ).astype(jnp.float32),
        lax.psum_scatter(
            totals[4].reshape(n_rows, -1).astype(jnp.bfloat16),
            "row",
            scatter_dimension=0,
            tiled=True,
        ).astype(jnp.float32),
        lax.psum_scatter(
            totals[5].reshape(n_rows, -1).astype(jnp.bfloat16),
            "row",
            scatter_dimension=0,
            tiled=True,
        ).astype(jnp.float32),
        lax.psum_scatter(
            totals[6].reshape(n_rows, -1).astype(jnp.bfloat16),
            "row",
            scatter_dimension=0,
            tiled=True,
        ).astype(jnp.float32),
    )
    shares = (
        lax.psum_scatter(
            first_pass[0].astype(jnp.bfloat16), "col", scatter_dimension=1, tiled=True
        ).astype(jnp.float32),
        lax.psum_scatter(
            first_pass[1].astype(jnp.bfloat16), "col", scatter_dimension=1, tiled=True
        ).astype(jnp.float32),
        lax.psum_scatter(
            first_pass[2].astype(jnp.bfloat16), "col", scatter_dimension=1, tiled=True
        ).astype(jnp.float32),
        lax.psum_scatter(
            first_pass[3].astype(jnp.bfloat16), "col", scatter_dimension=1, tiled=True
        ).astype(jnp.float32),
        lax.psum_scatter(
            first_pass[4].astype(jnp.bfloat16), "col", scatter_dimension=1, tiled=True
        ).astype(jnp.float32),
        lax.psum_scatter(
            first_pass[5].astype(jnp.bfloat16), "col", scatter_dimension=1, tiled=True
        ).astype(jnp.float32),
        lax.psum_scatter(
            first_pass[6].astype(jnp.bfloat16), "col", scatter_dimension=1, tiled=True
        ).astype(jnp.float32),
    )
    return (
        outputs.reshape(-1, width),
        grads_seq.reshape(-1, width),
        shares[0],
        shares[1],
        shares[2],
        shares[3],
        shares[4].reshape(-1),
        shares[5].reshape(-1),
        shares[6].reshape(-1),
    )


def solution(mesh):
    placed = (
        P(("row", "col"), None),
        P(("row", "col"), None),
        P("row", "col"),
        P("row", "col"),
        P("row", "col"),
        P("row", "col"),
        P(("row", "col")),
        P(("row", "col")),
        P(("row", "col")),
        P(("row", "col"), None),
    )
    return jax.shard_map(
        on_device,
        mesh=mesh,
        in_specs=placed,
        out_specs=(
            P(("row", "col"), None),
            P(("row", "col"), None),
            P("row", "col"),
            P("row", "col"),
            P("row", "col"),
            P("row", "col"),
            P(("row", "col")),
            P(("row", "col")),
            P(("row", "col")),
        ),
        check_vma=False,
    )
```

profile of v0, /device:TPU:0, one launch (start us, length us, event | category | flops | bytes accessed | tf_op | source)
XLA Modules:
  0.0 1428.3 jit_solution(5490411273386765580)
XLA Ops:
  8.7 8.9 all_gather.48
  17.7 14.1 all_gather.44
  33.4 18.2 %all-gather.24.cloned.1.call-done = bf16[128,4096]{1,0:T(8,128)(2,1)} async-done(((bf16[128,1024]{1,0:T(8,128)(2,1)}), bf16[128,4096]{1,0:T(8,128)(2,1)}) %all-gather.24.cloned.1.call-update) | async-done | bytes 1048592 | tf_op jit(solution)/shard_map/all_gather | solution.py:120
  53.8 5.9 all-reduce.7
  59.7 20.7 %all-gather.6 = bf16[8,1,128]{2,1,0:T(2,128)(2,1)S(1)} all-gather(bf16[1,1,128]{2,1,0:T(2,128)(2,1)S(1)} %bitcast.239), channel_id=3, replica_groups=mesh['row'=8,'col'=4] {'row'}, dimensions={0}, use_global_device_ids=true | all-gather | bytes 2304 | tf_op jit(solution)/shard_map/all_gather | solution.py:131
  80.4 16.5 %all-gather.7 = bf16[8,1,128]{2,1,0:T(2,128)(2,1)S(1)} all-gather(bf16[1,1,128]{2,1,0:T(2,128)(2,1)S(1)} %bitcast.238), channel_id=5, replica_groups=mesh['row'=8,'col'=4] {'row'}, dimensions={0}, use_global_device_ids=true | all-gather | bytes 2304 | tf_op jit(solution)/shard_map/all_gather | solution.py:133
  96.9 18.4 %all-gather.8 = bf16[8,1,128]{2,1,0:T(2,128)(2,1)S(1)} all-gather(bf16[1,1,128]{2,1,0:T(2,128)(2,1)S(1)} %bitcast.237), channel_id=7, replica_groups=mesh['row'=8,'col'=4] {'row'}, dimensions={0}, use_global_device_ids=true | all-gather | bytes 2304 | tf_op jit(solution)/shard_map/all_gather | solution.py:132
  115.3 87.1 %all-gather.16.cloned.1.call-done = bf16[1024,3072]{1,0:T(8,128)(2,1)} async-done(((bf16[128,3072]{1,0:T(8,128)(2,1)}), bf16[1024,3072]{1,0:T(8,128)(2,1)}) %all-gather.16.cloned.1.call-update) | async-done | bytes 6291472 | tf_op jit(solution)/shard_map/all_gather | solution.py:127
  202.4 124.7 %all-gather.22.cloned.1.call-done = bf16[4096,1024]{1,0:T(8,128)(2,1)} async-done(((bf16[512,1024]{1,0:T(8,128)(2,1)}), bf16[4096,1024]{1,0:T(8,128)(2,1)}) %all-gather.22.cloned.1.call-update) | async-done | bytes 8388624 | tf_op jit(solution)/shard_map/all_gather | solution.py:130
  327.0 124.7 %all-gather.26.cloned.1.call-done = bf16[1024,4096]{1,0:T(8,128)(2,1)} async-done(((bf16[128,4096]{1,0:T(8,128)(2,1)}), bf16[1024,4096]{1,0:T(8,128)(2,1)}) %all-gather.26.cloned.1.call-update) | async-done | bytes 8388624 | tf_op jit(solution)/shard_map/all_gather | solution.py:129
  451.7 307.4 %while.29 = (s32[]{:T(128)}, f32[1024,3072]{1,0:T(8,128)}, f32[1024,1024]{1,0:T(8,128)}, f32[1024,4096]{1,0:T(8,128)}, f32[4096,1024]{1,0:T(8,128)}, /*index=5*/...) while((s32[]{:T(128)}, f32[1024,3072]{1,0:T(8,128)}, ...), condition=%wide.region_13.15_spmd.clone, body=%wide.region_0.14_spmd.clone.sunk | while | flops 20289763328 | bytes 545137472 | solution.py:162
  461.8 5.9 convolution_convert_fusion.7
  478.2 12.9 fusion.175
  491.7 5.9 fusion.176
  502.8 6.8 fusion.177
  509.6 6.7 multiply_reduce_fusion.8
  537.3 9.6 scatter_custom_fusion.13
  546.9 8.4 bitcast_dynamic-update-slice_fusion.5
  555.7 9.9 select_add_fusion.15
  565.6 7.0 scatter_custom_fusion.12
  577.5 6.5 select_add_fusion.13
  586.7 8.3 select_add_fusion.16
  605.6 5.9 convolution_convert_fusion.7
  621.6 12.9 fusion.175
  635.1 5.9 fusion.176
  646.1 6.9 fusion.177
  653.0 6.7 multiply_reduce_fusion.8
  680.7 9.6 scatter_custom_fusion.13
  690.3 8.4 bitcast_dynamic-update-slice_fusion.5
  699.2 14.7 %select_add_fusion.15 = f32[1024,4096]{1,0:T(8,128)} fusion(f32[1024,4096]{1,0:T(8,128)} %get-tuple-element.602, bf16[256,4096]{1,0:T(8,128)(2,1)} %copy-done.16, pred[]{:T(512)S(6)} %compare.27, f32[256,1024]{1,0:T(8,128)S(1)} %get-tuple-element.558, f32[1024]{0:T(1024)S(1)} %get-tuple-element.639, f32[256]{0:T(256)S(1)} %add_rsqrt_fusion.5), kind=kOutput, calls=%fused_computation.6.clone.1 | convolution fusion | flops 2156658688 | bytes 36705280 | tf_op jit(solution)/shard_map/while/body/eval_jaxpr/dot_general | solution.py:69
  713.9 7.2 scatter_custom_fusion.12
  725.9 11.2 select_add_fusion.13
  742.2 14.1 select_add_fusion.16
  763.0 8.1 convert_element_type.189
  771.2 9.1 convert_element_type.193
  780.4 9.3 convert_element_type.195
  790.9 19.0 %all-reduce.6 = (bf16[8,128]{1,0:T(8,128)(2,1)S(1)}, bf16[8,128]{1,0:T(8,128)(2,1)S(1)}, bf16[8,128]{1,0:T(8,128)(2,1)S(1)}) all-reduce(bf16[8,128]{1,0:T(8,128)(2,1)S(1)} %convert_bitcast_fusion.2, bf16[8,128]{1,0:T(8,128)(2,1)S(1)} %get-tuple-element.407, ...), channel_id=16, replica_groups=mesh['row'=8,'col'=4] {'row'}, use_global_device_ids=true, to_apply=%region_22.24.clone | all-reduce | flops 3072 | bytes 12288
  814.3 15.5 %reduce-scatter.22.cloned.1.call-done = bf16[128,1024]{1,0:T(8,128)(2,1)} async-done(((bf16[1024,1024]{1,0:T(8,128)(2,1)}), bf16[128,1024]{1,0:T(8,128)(2,1)}) %reduce-scatter.22.cloned.1.call-update) | async-done | bytes 262160 | tf_op jit(solution)/shard_map/reduce_scatter | solution.py:172
  829.8 120.6 %reduce-scatter.18.cloned.1.call-done = bf16[128,3072]{1,0:T(8,128)(2,1)} async-done(((bf16[1024,3072]{1,0:T(8,128)(2,1)}), bf16[128,3072]{1,0:T(8,128)(2,1)}) %reduce-scatter.18.cloned.1.call-update) | async-done | bytes 786448 | tf_op jit(solution)/shard_map/reduce_scatter | solution.py:169
  950.5 150.3 %reduce-scatter.26.cloned.1.call-done = bf16[128,4096]{1,0:T(8,128)(2,1)} async-done(((bf16[1024,4096]{1,0:T(8,128)(2,1)}), bf16[128,4096]{1,0:T(8,128)(2,1)}) %reduce-scatter.26.cloned.1.call-update) | async-done | bytes 1048592 | tf_op jit(solution)/shard_map/reduce_scatter | solution.py:175
  1100.9 150.0 %reduce-scatter.30.cloned.1.call-done = bf16[512,1024]{1,0:T(8,128)(2,1)} async-done(((bf16[4096,1024]{1,0:T(8,128)(2,1)}), bf16[512,1024]{1,0:T(8,128)(2,1)}) %reduce-scatter.30.cloned.1.call-update) | async-done | bytes 1048592 | tf_op jit(solution)/shard_map/reduce_scatter | solution.py:178
  1250.9 21.6 %reduce-scatter.38.cloned.1.call-done = bf16[32,1]{1,0:T(8,128)(2,1)} async-done(((bf16[128,1]{1,0:T(8,128)(2,1)}), bf16[32,1]{1,0:T(8,128)(2,1)}) %reduce-scatter.38.cloned.1.call-update) | async-done | bytes 80
  1273.3 21.6 %reduce-scatter.36.cloned.1.call-done = bf16[32,1]{1,0:T(8,128)(2,1)} async-done(((bf16[128,1]{1,0:T(8,128)(2,1)}), bf16[32,1]{1,0:T(8,128)(2,1)}) %reduce-scatter.36.cloned.1.call-update) | async-done | bytes 80
  1295.6 21.7 %reduce-scatter.34.cloned.1.call-done = bf16[32,1]{1,0:T(8,128)(2,1)} async-done(((bf16[128,1]{1,0:T(8,128)(2,1)}), bf16[32,1]{1,0:T(8,128)(2,1)}) %reduce-scatter.34.cloned.1.call-update) | async-done | bytes 80
  1319.7 20.1 %reduce-scatter.24.cloned.1.call-done = bf16[128,256]{1,0:T(8,128)(2,1)} async-done(((bf16[128,1024]{1,0:T(8,128)(2,1)}), bf16[128,256]{1,0:T(8,128)(2,1)}) %reduce-scatter.24.cloned.1.call-update) | async-done | bytes 65552 | tf_op jit(solution)/shard_map/reduce_scatter | solution.py:204
  1341.3 24.1 %reduce-scatter.20.cloned.1.call-done = bf16[128,768]{1,0:T(8,128)(2,1)} async-done(((bf16[128,3072]{1,0:T(8,128)(2,1)}), bf16[128,768]{1,0:T(8,128)(2,1)}) %reduce-scatter.20.cloned.1.call-update) | async-done | bytes 196624 | tf_op jit(solution)/shard_map/reduce_scatter | solution.py:201
  1367.1 25.5 %reduce-scatter.28.cloned.1.call-done = bf16[128,1024]{1,0:T(8,128)(2,1)} async-done(((bf16[128,4096]{1,0:T(8,128)(2,1)}), bf16[128,1024]{1,0:T(8,128)(2,1)}) %reduce-scatter.28.cloned.1.call-update) | async-done | bytes 262160 | tf_op jit(solution)/shard_map/reduce_scatter | solution.py:207
  1394.4 25.4 %reduce-scatter.32.cloned.1.call-done = bf16[512,256]{1,0:T(8,128)(2,1)} async-done(((bf16[512,1024]{1,0:T(8,128)(2,1)}), bf16[512,256]{1,0:T(8,128)(2,1)}) %reduce-scatter.32.cloned.1.call-update) | async-done | bytes 262160 | tf_op jit(solution)/shard_map/reduce_scatter | solution.py:210
  (285 shorter events, 136.6 us)
Async XLA Ops:
  7.2 44.7 %copy-start.25 = (u32[32]{0:T(128)S(1)}, u32[32]{0:T(128)}, u32[]{:S(2)}) copy-start(u32[32]{0:T(128)} %constant.273) | copy-start | bytes 388
  7.2 45.9 %copy-start.21 = (bf16[32]{0:T(256)(128)(2,1)S(1)}, bf16[32]{0:T(256)(128)(2,1)}, u32[]{:S(2)}) copy-start(bf16[32]{0:T(256)(128)(2,1)} %param.20) | copy-start | bytes 196
  7.2 46.1 %copy-start.22 = (bf16[32]{0:T(256)(128)(2,1)S(1)}, bf16[32]{0:T(256)(128)(2,1)}, u32[]{:S(2)}) copy-start(bf16[32]{0:T(256)(128)(2,1)} %param.22) | copy-start | bytes 196
  7.2 46.4 %copy-start.23 = (bf16[32]{0:T(256)(128)(2,1)S(1)}, bf16[32]{0:T(256)(128)(2,1)}, u32[]{:S(2)}) copy-start(bf16[32]{0:T(256)(128)(2,1)} %param.21) | copy-start | bytes 196
  7.2 26.1 %all-gather.20.cloned.1.call-start = ((), (), s32[]{:S(2)}) async-start(), calls=%async_computation.13 | async-start | bytes 1310720 | tf_op jit(solution)/shard_map/all_gather | solution.py:121
  8.0 43.7 %all-gather.24.cloned.1.call-start = ((), (), s32[]{:S(2)}) async-start(), calls=%async_computation.15 | async-start | bytes 1310720 | tf_op jit(solution)/shard_map/all_gather | solution.py:120
  8.7 106.6 %all-gather.18.cloned.1.call-start = ((), (), s32[]{:S(2)}) async-start(), calls=%async_computation.12 | async-start | bytes 2359296 | tf_op jit(solution)/shard_map/all_gather | solution.py:128
  17.6 184.8 %all-gather.16.cloned.1.call-start = ((), (), s32[]{:S(2)}) async-start(), calls=%async_computation.11 | async-start | bytes 7077888 | tf_op jit(solution)/shard_map/all_gather | solution.py:127
  31.8 295.3 %all-gather.22.cloned.1.call-start = ((), (), s32[]{:S(2)}) async-start(), calls=%async_computation.14 | async-start | bytes 9437184 | tf_op jit(solution)/shard_map/all_gather | solution.py:130
  33.4 418.3 %all-gather.26.cloned.1.call-start = ((), (), s32[]{:S(2)}) async-start(), calls=%async_computation.16 | async-start | bytes 9437184 | tf_op jit(solution)/shard_map/all_gather | solution.py:129
  51.7 778.0 %reduce-scatter.22.cloned.1.call-start = ((), (), s32[]{:S(2)}) async-start(), calls=%async_computation.19 | async-start | bytes 2359296 | tf_op jit(solution)/shard_map/reduce_scatter | solution.py:172
  472.0 5.1 slice-start.4
  472.0 6.1 slice-start.5
  474.1 17.0 %copy-start.14 = (bf16[16,256,64]{1,2,0:T(8,128)(2,1)}, bf16[16,256,64]{1,2,0:T(8,128)(2,1)S(1)}, u32[]{:S(2)}) copy-start(bf16[16,256,64]{1,2,0:T(8,128)(2,1)S(1)} %convolution_convert_fusion.8) | copy-start | bytes 1572868 | tf_op jit(solution)/shard_map/while
  475.3 16.4 %slice-start = ((s8[8388608]{0:T(1024)(128)(4,1)}), s8[4194304]{0:T(1024)(128)(4,1)S(1)}, s32[]{:S(2)}) async-start(s8[8388608]{0:T(1024)(128)(4,1)} %bitcast.211), calls=%async_computation.28 | async-start | bytes 8388608 | tf_op jit(solution)/shard_map/while
  478.2 13.5 slice-start.1
  509.6 6.8 copy-start.16
  509.6 6.8 copy-start
  509.6 8.6 copy-start.11
  527.6 6.4 slice-start.6
  528.5 5.5 copy-start.2
  555.7 9.9 copy-start.18
  577.5 6.5 copy-start.13
  577.5 6.5 copy-start.15
  615.4 5.1 slice-start.4
  615.4 6.1 slice-start.5
  617.5 17.0 %copy-start.14 = (bf16[16,256,64]{1,2,0:T(8,128)(2,1)}, bf16[16,256,64]{1,2,0:T(8,128)(2,1)S(1)}, u32[]{:S(2)}) copy-start(bf16[16,256,64]{1,2,0:T(8,128)(2,1)S(1)} %convolution_convert_fusion.8) | copy-start | bytes 1572868 | tf_op jit(solution)/shard_map/while
  618.7 16.4 %slice-start = ((s8[8388608]{0:T(1024)(128)(4,1)}), s8[4194304]{0:T(1024)(128)(4,1)S(1)}, s32[]{:S(2)}) async-start(s8[8388608]{0:T(1024)(128)(4,1)} %bitcast.211), calls=%async_computation.28 | async-start | bytes 8388608 | tf_op jit(solution)/shard_map/while
  621.6 13.5 slice-start.1
  653.0 6.8 copy-start.16
  653.0 6.8 copy-start
  653.0 8.5 copy-start.11
  671.0 6.4 slice-start.6
  671.9 5.5 copy-start.2
  699.2 14.7 %copy-start.18 = (f32[256,1024]{1,0:T(8,128)S(1)}, f32[256,1024]{1,0:T(8,128)}, u32[]{:S(2)}) copy-start(f32[256,1024]{1,0:T(8,128)} %copy-done.17) | copy-start | bytes 3145732 | tf_op jit(solution)/shard_map/while
  725.9 11.2 copy-start.13
  725.9 11.2 copy-start.15
  737.1 5.1 copy-start.5
  763.0 187.5 %reduce-scatter.18.cloned.1.call-start = ((), (), s32[]{:S(2)}) async-start(), calls=%async_computation.17 | async-start | bytes 7077888 | tf_op jit(solution)/shard_map/reduce_scatter | solution.py:169
  771.1 329.7 %reduce-scatter.26.cloned.1.call-start = ((), (), s32[]{:S(2)}) async-start(), calls=%async_computation.21 | async-start | bytes 9437184 | tf_op jit(solution)/shard_map/reduce_scatter | solution.py:175
  780.3 470.6 %reduce-scatter.30.cloned.1.call-start = ((), (), s32[]{:S(2)}) async-start(), calls=%async_computation.23 | async-start | bytes 9437184 | tf_op jit(solution)/shard_map/reduce_scatter | solution.py:178
  789.7 482.8 %reduce-scatter.38.cloned.1.call-start = ((), (), s32[]{:S(2)}) async-start(), calls=%async_computation.27 | async-start | bytes 40960
  811.3 483.6 %reduce-scatter.36.cloned.1.call-start = ((), (), s32[]{:S(2)}) async-start(), calls=%async_computation.26 | async-start | bytes 40960
  812.8 504.6 %reduce-scatter.34.cloned.1.call-start = ((), (), s32[]{:S(2)}) async-start(), calls=%async_computation.25 | async-start | bytes 40960
  814.2 525.5 %reduce-scatter.24.cloned.1.call-start = ((), (), s32[]{:S(2)}) async-start(), calls=%async_computation.20 | async-start | bytes 327680 | tf_op jit(solution)/shard_map/reduce_scatter | solution.py:204
  829.8 535.6 %reduce-scatter.20.cloned.1.call-start = ((), (), s32[]{:S(2)}) async-start(), calls=%async_computation.18 | async-start | bytes 983040 | tf_op jit(solution)/shard_map/reduce_scatter | solution.py:201
  950.5 442.1 %reduce-scatter.28.cloned.1.call-start = ((), (), s32[]{:S(2)}) async-start(), calls=%async_computation.22 | async-start | bytes 1310720 | tf_op jit(solution)/shard_map/reduce_scatter | solution.py:207
  1100.9 318.9 %reduce-scatter.32.cloned.1.call-start = ((), (), s32[]{:S(2)}) async-start(), calls=%async_computation.24 | async-start | bytes 1310720 | tf_op jit(solution)/shard_map/reduce_scatter | solution.py:210
  (32 other events, 81.0 us)
Sparse Core Ops, SparseCore 0:
  9.6 23.7 all-gather.19
  34.9 16.6 all-gather.23
  53.8 49.2 all-gather.17
  105.1 97.2 all-gather.15
  204.4 122.6 all-gather.21
  329.0 122.6 all-gather.25
  763.1 66.5 reduce-scatter.21
  833.3 117.0 reduce-scatter.17
  954.1 146.7 reduce-scatter.25
  1104.3 146.5 reduce-scatter.29
  1253.9 18.5 reduce-scatter.37
  1275.3 19.4 reduce-scatter.35
  1297.8 19.4 reduce-scatter.33
  1319.7 20.0 reduce-scatter.23
  1342.1 23.1 reduce-scatter.19
  1367.8 24.7 reduce-scatter.27
  1395.0 24.7 reduce-scatter.31
where the time goes:
time: 1430 us
  waiting for transfers between devices  954 us (67%)
  matrix products  170 us (12%)
  blocking collectives  103 us (7%)
  other arithmetic  91.8 us (6%)
  local copies, waits for them, and re-layouts  89.2 us (6%)
  between operations  15.1 us (1%)
    reduce_scatter x1, waiting for transfers between devices, on_device(): lax.psum_scatter(totals[2].astype(jnp.bfloat16), 'row', scatter_dimension...  150 us
    reduce_scatter x1, waiting for transfers between devices, on_device(): lax.psum_scatter(totals[3].astype(jnp.bfloat16), 'row', scatter_dimension...  150 us
    all_gather x1, waiting for transfers between devices, on_device(): lax.all_gather(across[2], 'row', axis=0, tiled=True)  125 us
    all_gather x1, waiting for transfers between devices, on_device(): lax.all_gather(across[3], 'row', axis=0, tiled=True)  125 us
    reduce_scatter x1, waiting for transfers between devices, on_device(): lax.psum_scatter(totals[0].astype(jnp.bfloat16), 'row', scatter_dimension...  121 us
    all_gather x1, waiting for transfers between devices, on_device(): lax.all_gather(across[0], 'row', axis=0, tiled=True)  87.1 us
    unnamed x20, waiting for transfers between devices  66.5 us
  transfers between devices with their start and end apart: 17, of which 16 were waited for; matrix products, arithmetic and copies ran while one was open for 3% of the time, Pallas kernels for 0%

commit v1 on v0

v1 whole, which is shorter than its diff:
```python
import jax
import jax.numpy as jnp
from jax import lax
from jax.sharding import PartitionSpec as P

HEADS = 16
HEAD_DIM = 64
L = 2048
BLOCK = 256

epsilon = 1e-05
sqrt_half = 0.7071067811865476
inv_root_two_pi = 0.3989422804014327

BOTH = ("row", "col")
F32 = jnp.float32
BF16 = jnp.bfloat16


def phi_parts(z):
    cdf = 0.5 * (1.0 + lax.erf(z * sqrt_half))
    slope = cdf + z * jnp.exp(-0.5 * z * z) * inv_root_two_pi
    return cdf, slope


def gather_weight(shard):
    rows, cols = lax.axis_size("row"), lax.axis_size("col")
    blocks = lax.all_gather(shard, BOTH, axis=0, tiled=False)
    high, wide = shard.shape
    blocks = blocks.reshape(rows, cols, high, wide).transpose(0, 2, 1, 3)
    return blocks.reshape(rows * high, cols * wide)


def scatter_grad(grad):
    rows, cols = lax.axis_size("row"), lax.axis_size("col")
    high, wide = grad.shape[0] // rows, grad.shape[1] // cols
    blocks = grad.reshape(rows, high, cols, wide).transpose(0, 2, 1, 3)
    blocks = blocks.reshape(rows * cols * high, wide)
    mine = lax.psum_scatter(blocks, BOTH, scatter_dimension=0, tiled=True)
    return mine.astype(F32)


def dot(left, right):
    return jnp.dot(left, right, preferred_element_type=F32)


def dot_t(left, right):
    return lax.dot_general(left, right, (((1,), (1,)), ((), ())), preferred_element_type=F32)


def t_dot(left, right):
    return lax.dot_general(left, right, (((0,), (0,)), ((), ())), preferred_element_type=F32)


def on_device(hidden, routes, w_qkv, w_proj, w_up, w_down, attn_gain, mlp_gain, router, cotangent):
    n_dev = lax.axis_size("row") * lax.axis_size("col")
    width = hidden.shape[1]
    seqs = hidden.shape[0] // L
    cap = routes.shape[1]
    tokens = seqs * cap
    scale = HEAD_DIM ** (-0.5)

    small = jnp.stack([attn_gain, mlp_gain, router])
    small = lax.all_gather(small, BOTH, axis=1, tiled=True).astype(F32)
    gain_attn, gain_mlp, router_vec = small[0], small[1], small[2]
    qkv_mat = gather_weight(w_qkv)
    proj_mat = gather_weight(w_proj)
    up_mat = gather_weight(w_up)
    down_mat = gather_weight(w_down)

    picks = (routes[:, :, None] == lax.broadcasted_iota(jnp.int32, (1, 1, L), 2)).astype(BF16)
    hidden3 = hidden.reshape(seqs, L, width)
    cot3 = cotangent.reshape(seqs, L, width)
    is_routed = jnp.sum(picks, axis=1, dtype=F32) > 0.5
    x = jnp.einsum("scl,sld->scd", picks, hidden3, preferred_element_type=F32).reshape(tokens, width)
    g = jnp.einsum("scl,sld->scd", picks, cot3, preferred_element_type=F32).reshape(tokens, width)

    gate = jax.nn.sigmoid(jnp.sum(x * router_vec, axis=-1, keepdims=True))
    r1 = lax.rsqrt(jnp.mean(x * x, axis=-1, keepdims=True) + epsilon)
    n1 = x * r1
    a = (n1 * gain_attn).astype(BF16)
    qkv = dot(a, qkv_mat).astype(BF16)
    split = qkv.reshape(seqs, cap, 3, HEADS, HEAD_DIM).transpose(2, 0, 3, 1, 4)
    q, k, v = split[0], split[1], split[2]
    scores = jnp.einsum("shqd,shkd->shqk", q, k, preferred_element_type=F32) * scale
    blocks = routes // BLOCK
    allowed = blocks[:, :, None] >= blocks[:, None, :]
    masked = jnp.where(allowed[:, None], scores, -1e30)
    expo = jnp.exp(masked - jnp.max(masked, axis=-1, keepdims=True))
    probs = expo / jnp.sum(expo, axis=-1, keepdims=True)
    probs_low = probs.astype(BF16)
    mixed = jnp.einsum("shqk,shkd->shqd", probs_low, v, preferred_element_type=F32).astype(BF16)
    mixed = mixed.transpose(0, 2, 1, 3).reshape(tokens, width)
    attn = dot(mixed, proj_mat)
    u = x + attn
    r2 = lax.rsqrt(jnp.mean(u * u, axis=-1, keepdims=True) + epsilon)
    n2 = u * r2
    b = (n2 * gain_mlp).astype(BF16)
    z = dot(b, up_mat)
    cdf, slope = phi_parts(z)
    act = (z * cdf).astype(BF16)
    gmlp = (gate * g).astype(BF16)
    d_down = t_dot(act, gmlp).astype(BF16)
    out_down = scatter_grad(d_down)

    gz = (dot_t(gmlp, down_mat) * slope).astype(BF16)
    d_up = t_dot(b, gz).astype(BF16)
    out_up = scatter_grad(d_up)
    mlp = dot(act, down_mat)
    branch = attn + mlp
    gscore = jnp.sum(g * branch, axis=-1, keepdims=True) * gate * (1.0 - gate)

    gb = dot_t(gz, up_mat)
    t = gb * gain_mlp
    gu = r2 * (t - n2 * jnp.mean(t * n2, axis=-1, keepdims=True))
    gattn = (gate * g + gu).astype(BF16)
    d_proj = t_dot(mixed, gattn).astype(BF16)
    out_proj = scatter_grad(d_proj)
    gheads = dot_t(gattn, proj_mat).astype(BF16)
    gheads = gheads.reshape(seqs, cap, HEADS, HEAD_DIM).transpose(0, 2, 1, 3)
    gprobs = jnp.einsum("shqd,shkd->shqk", gheads, v, preferred_element_type=F32)
    gv = jnp.einsum("shqk,shqd->shkd", probs_low, gheads, preferred_element_type=F32)
    gs = (probs * (gprobs - jnp.sum(probs * gprobs, axis=-1, keepdims=True))).astype(BF16)
    gq = jnp.einsum("shqk,shkd->shqd", gs, k, preferred_element_type=F32) * scale
    gk = jnp.einsum("shqk,shqd->shkd", gs, q, preferred_element_type=F32) * scale
    gqkv = jnp.stack([gq, gk, gv]).astype(BF16).transpose(1, 3, 0, 2, 4).reshape(tokens, 3 * width)
    d_qkv = t_dot(a, gqkv).astype(BF16)
    out_qkv = scatter_grad(d_qkv)

    ga = dot_t(gqkv, qkv_mat)
    t1 = ga * gain_attn
    gx = g + gscore * router_vec + gu + r1 * (t1 - n1 * jnp.mean(t1 * n1, axis=-1, keepdims=True))
    small_grads = jnp.stack(
        [jnp.sum(ga * n1, axis=0), jnp.sum(gb * n2, axis=0), jnp.sum(gscore * x, axis=0)]
    )
    small_grads = small_grads.reshape(3, n_dev, width // n_dev).transpose(1, 0, 2)
    small_grads = lax.psum_scatter(
        small_grads.reshape(n_dev, 3 * (width // n_dev)), BOTH, scatter_dimension=0, tiled=True
    ).reshape(3, width // n_dev)

    updated = (x + gate * branch).astype(BF16).reshape(seqs, cap, width)
    placed = jnp.einsum("scl,scd->sld", picks, updated, preferred_element_type=F32).astype(BF16)
    layer_out = jnp.where(is_routed[:, :, None], placed, hidden3)
    gx_high = gx.astype(BF16)
    gx_low = (gx - gx_high.astype(F32)).astype(BF16)
    back = jnp.einsum(
        "scl,scd->sld", picks, gx_high.reshape(seqs, cap, width), preferred_element_type=F32
    ) + jnp.einsum("scl,scd->sld", picks, gx_low.reshape(seqs, cap, width), preferred_element_type=F32)
    grad_hidden = jnp.where(is_routed[:, :, None], back, cot3.astype(F32))
    return (
        layer_out.reshape(-1, width),
        grad_hidden.reshape(-1, width),
        out_qkv,
        out_proj,
        out_up,
        out_down,
        small_grads[0],
        small_grads[1],
        small_grads[2],
    )


def solution(mesh):
    rowcol = P(BOTH, None)
    weight = P("row", "col")
    vector = P(BOTH)
    return jax.shard_map(
        on_device,
        mesh=mesh,
        in_specs=(rowcol, rowcol, weight, weight, weight, weight, vector, vector, vector, rowcol),
        out_specs=(rowcol, rowcol, weight, weight, weight, weight, vector, vector, vector),
        check_vma=False,
    )
```

time: 1430 us -> 949 us (0.66)
  waiting for transfers between devices: 954 us -> 519 us
  local copies, waits for them, and re-layouts: 89.2 us -> 159 us
  other arithmetic: 91.8 us -> 24.2 us
  matrix products: 170 us -> 141 us
  blocking collectives: 103 us -> 82.9 us
    all_gather x6 -> x4, waiting for transfers between devices: 356 us -> 164 us  [gather_weight(): blocks = lax.all_gather(shard, BOTH, axis=0, tiled=False)]
    reduce_scatter x8 -> x4, waiting for transfers between devices: 531 us -> 352 us  [scatter_grad(): mine = lax.psum_scatter(blocks, BOTH, scatter_dimension=0, tiled=True)]
    reshape x0 -> x12, local copies, waits for them, and re-layouts: none -> 105 us  [the longest x4 46 us: scatter_grad(): blocks = grad.reshape(rows, high, cols, wide).transpose(0, 2, 1, 3)]
    unnamed x20 -> x8, waiting for transfers between devices: 66.5 us -> 2.65 us
    convert_element_type x19 -> x9, other arithmetic: 51.6 us -> 11.3 us  [the longest x4 6.77 us: scatter_grad(): return mine.astype(F32)]
    all_gather x5 -> x1, blocking collectives: 78.5 us -> 43.3 us  [on_device(): small = lax.all_gather(small, BOTH, axis=1, tiled=True).astype(F32)]
    scatter x4 -> x0, other arithmetic: 33.5 us -> none  [the longest x2 19.2 us: one_sequence(): grad_sequence = seq_cot.astype(jnp.float32).at[picked].set(grad_rows)]
    transpose x0 -> x5, local copies, waits for them, and re-layouts: none -> 31.5 us  [the longest x4 28.2 us: scatter_grad(): blocks = grad.reshape(rows, high, cols, wide).transpose(0, 2, 1, 3)]
  transfers between devices with their start and end apart: 17 -> 8, of which waited for: 16 -> 7; matrix products, arithmetic and copies ran while one was open for 3% -> 25% of each run, Pallas kernels for 0% -> 0%
where the time goes in v1:
time: 949 us; the launch traced here: 942 us
  waiting for transfers between devices  519 us (55%)
  local copies, waits for them, and re-layouts  159 us (17%)
  matrix products  141 us (15%)
  blocking collectives  82.9 us (9%)
  other arithmetic  24.2 us (3%)
  between operations  14.9 us (2%)
    reduce_scatter x4, waiting for transfers between devices, scatter_grad(): mine = lax.psum_scatter(blocks, BOTH, scatter_dimension=0, tiled=True)  352 us
    all_gather x4, waiting for transfers between devices, gather_weight(): blocks = lax.all_gather(shard, BOTH, axis=0, tiled=False)  164 us
    reshape x4, local copies, waits for them, and re-layouts, scatter_grad(): blocks = grad.reshape(rows, high, cols, wide).transpose(0, 2, 1, 3)  46 us
    all_gather x1, blocking collectives, on_device(): small = lax.all_gather(small, BOTH, axis=1, tiled=True).astype(F32)  43.3 us
    reshape x4, local copies, waits for them, and re-layouts, gather_weight(): blocks = blocks.reshape(rows, cols, high, wide).transpose(0, 2, 1, 3)  41 us
    unnamed x1, blocking collectives  39.6 us
    dot_general x4, matrix products, dot(): return jnp.dot(left, right, preferred_element_type=F32)  29.9 us
    transpose x4, local copies, waits for them, and re-layouts, scatter_grad(): blocks = grad.reshape(rows, high, cols, wide).transpose(0, 2, 1, 3)  28.2 us
  transfers between devices with their start and end apart: 8, of which 7 were waited for; matrix products, arithmetic and copies ran while one was open for 25% of the time, Pallas kernels for 0%

profile of v1, /device:TPU:0, one launch (start us, length us, event | category | flops | bytes accessed | tf_op | source)
XLA Modules:
  0.0 941.6 jit_solution(5800509005951092322)
XLA Ops:
  10.7 43.3 %all-gather.4 = bf16[32,32,3]{1,2,0:T(4,128)(2,1)S(1)} all-gather(bf16[1,32,3]{1,2,0:T(4,128)(2,1)S(1)} %maximum_bitcast_fusion.2), channel_id=1, replica_groups=mesh['row'=8,'col'=4] {'row','col'}, dimensions={0}, use_global_device_ids=true | all-gather | bytes 6336 | tf_op jit(solution)/shard_map/all_gather | solution.py:64
  54.9 6.0 multiply_reduce_fusion.8
  61.9 7.5 fusion.26
  69.8 4.8 copy.82
  74.6 66.1 %all-gather.10.cloned.1.call-done = bf16[4096,768]{1,0:T(8,128)(2,1)} async-done(((bf16[128,768]{1,0:T(8,128)(2,1)}), bf16[4096,768]{1,0:T(8,128)(2,1)}) %all-gather.10.cloned.1.call-update) | async-done | bytes 6291472 | tf_op jit(solution)/shard_map/all_gather | solution.py:28
  140.7 9.0 copy.77
  149.8 7.8 fusion.20
  157.5 8.5 reshape.277
  166.1 8.2 copy.79
  174.3 2.8 fusion.68
  177.1 2.4 fusion.75
  179.5 3.0 fusion.62
  184.4 3.3 multiply_reduce_fusion.6
  187.7 31.5 %all-gather.14.cloned.1.call-done = bf16[4096,1024]{1,0:T(8,128)(2,1)} async-done(((bf16[128,1024]{1,0:T(8,128)(2,1)}), bf16[4096,1024]{1,0:T(8,128)(2,1)}) %all-gather.14.cloned.1.call-update) | async-done | bytes 8388624 | tf_op jit(solution)/shard_map/all_gather | solution.py:28
  219.2 12.4 %copy.83 = bf16[8,4,128,1024]{2,0,3,1:T(8,128)(2,1)} copy(bf16[8,4,128,1024]{3,2,1,0:T(8,128)(2,1)} %bitcast.203) | data formatting | bytes 16777216 | tf_op jit(solution)/shard_map/reshape | solution.py:30
  231.6 66.0 %all-gather.16.cloned.1.call-done = bf16[16384,256]{1,0:T(8,128)(2,1)} async-done(((bf16[512,256]{1,0:T(8,128)(2,1)}), bf16[16384,256]{1,0:T(8,128)(2,1)}) %all-gather.16.cloned.1.call-update) | async-done | bytes 8388624 | tf_op jit(solution)/shard_map/all_gather | solution.py:28
  297.6 14.7 %copy.84 = bf16[8,4,512,256]{2,0,3,1:T(8,128)(2,1)} copy(bf16[8,4,512,256]{3,2,1,0:T(8,128)(2,1)} %bitcast.204) | data formatting | bytes 16777216 | tf_op jit(solution)/shard_map/reshape | solution.py:30
  312.3 12.3 %copy.110 = bf16[128,8,8,512]{3,1,2,0:T(8,128)(2,1)} copy(bf16[128,8,8,512]{3,2,1,0:T(8,128)(2,1)} %bitcast.185) | data formatting | bytes 16777216
  324.7 10.7 %multiply_convert_fusion.1 = (bf16[512,4096]{1,0:T(8,128)(2,1)}, f32[512,4096]{1,0:T(8,128)}) fusion(bf16[512,8,8,128]{3,2,1,0:T(8,128)(2,1)} %bitcast.205, f32[512,1024]{1,0:T(8,128)S(1)} %copy-done.2, f32[1024]{0:T(1024)S(1)} %bitcast.231, f32[512]{0:T(512)S(1)} %add_rsqrt_fusion), kind=kOutput, calls=%fused_computation.16 | convolution fusion | flops 4307025920 | bytes 23074816 | tf_op jit(solution)/shard_map/dot_general | solution.py:44
  335.4 8.2 fusion.34
  343.6 2.1 multiply_reduce_fusion.1
  345.7 10.4 %fusion.6 = bf16[512,4096]{1,0:T(8,128)(2,1)S(1)} fusion(f32[512,4096]{1,0:T(8,128)} %get-tuple-element.38, bf16[512,1024]{1,0:T(8,128)(2,1)S(1)} %bitcast.225, bf16[4096,1024]{0,1:T(8,128)(2,1)} %bitcast.209), kind=kOutput, calls=%fused_computation.8 | convolution fusion | flops 4315938816 | bytes 22020096 | tf_op jit(solution)/shard_map/dot_general | solution.py:48
  356.2 4.8 multiply_reduce_fusion.2
  363.7 2.2 fusion.56
  365.9 2.6 convolution_convert_fusion.3
  371.2 4.5 reshape.259
  375.7 3.5 copy.94
  379.2 5.4 multiply_reduce_fusion
  385.4 2.2 multiply_convert_fusion
  391.7 3.3 copy.92
  397.4 5.4 convolution_convert_fusion.2
  402.7 12.3 %reshape.257 = bf16[8,128,4,768]{3,2,1,0:T(4,128)(2,1)} reshape(bf16[1024,3072]{1,0:T(8,128)(2,1)} %convolution_convert_fusion.2) | data formatting | bytes 12582912 | tf_op jit(solution)/shard_map/reshape | solution.py:37
  415.1 6.7 copy.93
  423.0 9.2 convolution_convert_fusion
  432.2 14.5 %reshape.263 = bf16[8,512,4,256]{3,2,1,0:T(4,128)(2,1)} reshape(bf16[4096,1024]{1,0:T(8,128)(2,1)} %convolution_convert_fusion) | data formatting | bytes 16777216 | tf_op jit(solution)/shard_map/reshape | solution.py:37
  446.7 8.2 copy.96
  455.0 10.9 %convolution_convert_fusion.1 = bf16[1024,4096]{1,0:T(8,128)(2,1)} fusion(bf16[512,4096]{1,0:T(8,128)(2,1)} %copy-done.23, f32[512,1024]{1,0:T(8,128)} %get-tuple-element.20, f32[1024]{0:T(1024)S(1)} %bitcast.234, f32[512]{0:T(512)S(1)} %add_rsqrt_fusion), kind=kOutput, calls=%fused_computation.21 | convolution fusion | flops 4300734464 | bytes 14686208 | tf_op jit(solution)/shard_map/dot_general | solution.py:52
  465.9 14.7 %reshape.261 = bf16[8,128,4,1024]{3,2,1,0:T(4,128)(2,1)} reshape(bf16[1024,4096]{1,0:T(8,128)(2,1)} %convolution_convert_fusion.1) | data formatting | bytes 16777216 | tf_op jit(solution)/shard_map/reshape | solution.py:37
  480.6 9.8 %copy.95 = bf16[8,4,128,1024]{3,2,1,0:T(8,128)(2,1)} copy(bf16[8,4,128,1024]{3,1,2,0:T(4,128)(2,1)} %bitcast.187) | data formatting | bytes 16777216 | tf_op jit(solution)/shard_map/transpose | solution.py:37
  492.0 8.7 multiply_reduce_fusion.3
  500.9 39.6 %all-reduce = f32[32,96]{1,0:T(8,128)S(1)} all-reduce(f32[32,96]{1,0:T(8,128)S(1)} %reshape.265), channel_id=10, replica_groups=mesh['row'=8,'col'=4] {'row','col'}, use_global_device_ids=true, to_apply=%region_17.18.clone | all-reduce | flops 3072 | bytes 24576
  541.1 5.2 fusion.36
  546.7 8.5 fusion.25
  555.2 4.7 convert_select_fusion.1
  559.9 15.9 %convert_select_fusion = f32[2,2048,1024]{2,1,0:T(8,128)} fusion(bf16[2,2048,1024]{2,1,0:T(8,128)(2,1)} %bitcast.198, f32[2,2048,1024]{2,1,0:T(8,128)} %fusion.25, pred[2,2048]{1,0:T(4,128)(4,1)S(1)} %broadcast_compare_fusion.1, bf16[2,256,1024]{2,1,0:T(8,128)(2,1)S(1)} %bitcast.218, s32[2,256]{1,0:T(2,128)S(1)} %copy-done.17), kind=kOutput, calls=%fused_computation.1 | convolution fusion | flops 2161115136 | bytes 42997760 | tf_op jit(solution)/shard_map/scl,scd->sld/dot_general | solution.py:148
  577.3 55.1 %reduce-scatter.5.cloned.1.call-done = bf16[128,768]{1,0:T(8,128)(2,1)} async-done(((bf16[4096,768]{1,0:T(8,128)(2,1)}), bf16[128,768]{1,0:T(8,128)(2,1)}) %reduce-scatter.5.cloned.1.call-update) | async-done | bytes 196624 | tf_op jit(solution)/shard_map/reduce_scatter | solution.py:39
  634.1 150.1 %reduce-scatter.11.cloned.1.call-done = bf16[512,256]{1,0:T(8,128)(2,1)} async-done(((bf16[16384,256]{1,0:T(8,128)(2,1)}), bf16[512,256]{1,0:T(8,128)(2,1)}) %reduce-scatter.11.cloned.1.call-update) | async-done | bytes 262160 | tf_op jit(solution)/shard_map/reduce_scatter | solution.py:39
  785.9 146.8 %reduce-scatter.9.cloned.1.call-done = bf16[128,1024]{1,0:T(8,128)(2,1)} async-done(((bf16[4096,1024]{1,0:T(8,128)(2,1)}), bf16[128,1024]{1,0:T(8,128)(2,1)}) %reduce-scatter.9.cloned.1.call-update) | async-done | bytes 262160 | tf_op jit(solution)/shard_map/reduce_scatter | solution.py:39
  (121 shorter events, 31.0 us)
Async XLA Ops:
  7.2 62.6 %all-gather.12.cloned.1.call-start = ((), (), s32[]{:S(2)}) async-start(), calls=%async_computation.9 | async-start | bytes 2162688 | tf_op jit(solution)/shard_map/all_gather | solution.py:28
  7.9 132.8 %all-gather.10.cloned.1.call-start = ((), (), s32[]{:S(2)}) async-start(), calls=%async_computation.8 | async-start | bytes 6488064 | tf_op jit(solution)/shard_map/all_gather | solution.py:28
  8.7 210.5 %all-gather.14.cloned.1.call-start = ((), (), s32[]{:S(2)}) async-start(), calls=%async_computation.10 | async-start | bytes 8650752 | tf_op jit(solution)/shard_map/all_gather | solution.py:28
  9.4 288.2 %all-gather.16.cloned.1.call-start = ((), (), s32[]{:S(2)}) async-start(), calls=%async_computation.11 | async-start | bytes 8650752 | tf_op jit(solution)/shard_map/all_gather | solution.py:28
  10.0 565.8 %reduce-scatter.7.cloned.1.call-start = ((), (), s32[]{:S(2)}) async-start(), calls=%async_computation.5 | async-start | bytes 2162688 | tf_op jit(solution)/shard_map/reduce_scatter | solution.py:39
  54.9 6.0 copy-start.20
  54.9 6.8 copy-start.18
  54.9 7.0 copy-start.16
  61.9 87.8 %copy-start.12 = (bf16[2,256,1024]{2,1,0:T(8,128)(2,1)}, bf16[2,256,1024]{2,1,0:T(8,128)(2,1)S(1)}, u32[]{:S(2)}) copy-start(bf16[2,256,1024]{2,1,0:T(8,128)(2,1)S(1)} %multiply_convert_fusion.6) | copy-start | bytes 3145732
  179.5 3.3 copy-start.7
  182.8 1.6 copy-start.5
  312.3 12.4 %copy-start.2 = (f32[512,1024]{1,0:T(8,128)S(1)}, f32[512,1024]{1,0:T(8,128)}, u32[]{:S(2)}) copy-start(f32[512,1024]{1,0:T(8,128)} %get-tuple-element.20) | copy-start | bytes 6291460
  324.7 10.7 %copy-start = (f32[2,256,1024]{2,1,0:T(8,128)S(1)}, f32[2,256,1024]{2,1,0:T(8,128)}, u32[]{:S(2)}) copy-start(f32[2,256,1024]{2,1,0:T(8,128)} %fusion.26) | copy-start | bytes 6291460
  324.7 10.7 %copy-start.8 = (bf16[128,8,8,512]{3,1,2,0:T(8,128)(2,1)S(1)}, bf16[128,8,8,512]{3,1,2,0:T(8,128)(2,1)}, u32[]{:S(2)}) copy-start(bf16[128,8,8,512]{3,1,2,0:T(8,128)(2,1)} %copy.110) | copy-start | bytes 25165828
  324.7 10.7 %copy-start.11 = (f32[512,1024]{1,0:T(8,128)S(1)}, f32[512,1024]{1,0:T(8,128)}, u32[]{:S(2)}) copy-start(f32[512,1024]{1,0:T(8,128)} %get-tuple-element.36) | copy-start | bytes 6291460
  343.6 12.5 %slice-start.2 = ((s8[8388608]{0:T(1024)(128)(4,1)}), s8[4194304]{0:T(1024)(128)(4,1)S(1)}, s32[]{:S(2)}) async-start(s8[8388608]{0:T(1024)(128)(4,1)} %bitcast.206), calls=%async_computation.14 | async-start | bytes 8388608
  345.7 10.5 %copy-start.3 = (f32[512,1024]{1,0:T(8,128)S(1)}, f32[512,1024]{1,0:T(8,128)}, u32[]{:S(2)}) copy-start(f32[512,1024]{1,0:T(8,128)} %get-tuple-element.20) | copy-start | bytes 6291460
  345.7 10.5 %slice-start.3 = ((s8[8388608]{0:T(1024)(128)(4,1)}), s8[4194304]{0:T(1024)(128)(4,1)S(1)}, s32[]{:S(2)}) async-start(s8[8388608]{0:T(1024)(128)(4,1)} %bitcast.206), calls=%async_computation.15 | async-start | bytes 8388608
  356.2 4.8 copy-start.23
  356.2 4.8 copy-start.1
  361.0 1.7 copy-start.9
  361.0 2.7 copy-start.6
  375.7 3.5 copy-start.14
  379.1 253.2 %reduce-scatter.5.cloned.1.call-start = ((), (), s32[]{:S(2)}) async-start(), calls=%async_computation.4 | async-start | bytes 6488064 | tf_op jit(solution)/shard_map/reduce_scatter | solution.py:39
  379.2 5.4 slice-start
  379.2 6.2 slice-start.1
  385.4 2.2 copy-start.4
  395.0 2.4 copy-start.13
  395.7 1.7 copy-start.10
  421.8 1.2 copy-start.15
  421.8 362.3 %reduce-scatter.11.cloned.1.call-start = ((), (), s32[]{:S(2)}) async-start(), calls=%async_computation.7 | async-start | bytes 8650752 | tf_op jit(solution)/shard_map/reduce_scatter | solution.py:39
  454.9 477.8 %reduce-scatter.9.cloned.1.call-start = ((), (), s32[]{:S(2)}) async-start(), calls=%async_computation.6 | async-start | bytes 8650752 | tf_op jit(solution)/shard_map/reduce_scatter | solution.py:39
  490.4 0.7 copy-start.22
  490.4 0.7 copy-start.17
  490.4 1.5 copy-start.19
  491.9 49.1 %copy-start.21 = (f32[1,1024]{1,0:T(1,128)S(1)}, f32[1,1024]{1,0:T(1,128)}, u32[]{:S(2)}) copy-start(f32[1,1024]{1,0:T(1,128)} %copy-done.20) | copy-start | bytes 12292
  541.1 14.2 %slice-start.4 = ((s8[8388608]{0:T(1024)(128)(4,1)}), s8[4194304]{0:T(1024)(128)(4,1)S(1)}, s32[]{:S(2)}) async-start(s8[8388608]{0:T(1024)(128)(4,1)} %bitcast.251), calls=%async_computation.16 | async-start | bytes 8388608
  546.3 8.9 slice-start.5
Sparse Core Ops, SparseCore 0:
  10.8 58.9 all-gather.11
  72.7 67.9 all-gather.9
  143.6 75.5 all-gather.13
  221.9 75.6 all-gather.15
  379.3 136.6 reduce-scatter.6
  521.5 110.8 reduce-scatter.4
  634.7 149.4 reduce-scatter.10
  786.4 146.2 reduce-scatter.8
